TPU v7x, 32 devices: a whole 2x2x4 slice. The times are simulated.
32 devices in a mesh: ens: 4 (over y, x), slab: 8 (over z, core).
Axes of the slice: x: 2, y: 2, z: 4, core: 2. Of those that a mesh axis runs over, the one named last changes fastest.
Arguments:
- velocity: float32 [4, 3, 8, 2048, 1024], P('ens', None, None, 'slab'), may hold values from -6 to 6
- cutoffs: int32 [4, 2, 8], P('ens'), may hold values from 128 to 511, as said below
- plane_index: int32 [4], P('ens'), may hold values from 0 to 2047
- boundary_index: int32 [4], P('ens'), may hold values from 0 to 2047
Outputs:
- blended: float32 [4, 3, 8, 2048, 1024], P('ens', None, None, 'slab')
Inputs may be any that keep to these rules, and one draw needn't show every extreme that they name: `cutoffs`: row 0 lies in 256 to 511 and row 1 in 128 to 255; in every member some level has row 0 equal to 511 and some level has row 1 equal to 255.
All inputs are finite; a program needn't handle non-finite values.
Results may differ from a plain program's by a relative error of at most 0.0003.
Values sent between devices are 32-bit elements; how exact they have to be, the bound alone decides.
A program may use at most 128 MiB of HBM per device.

v0:
```python
import math
import jax
import jax.numpy as jnp
from jax import lax
from jax.sharding import PartitionSpec as P

KX = 512
KY = 256
highest = lax.Precision.HIGHEST


def spread(value, axis, source):
    kept = jnp.where(lax.axis_index(axis) == source, value, 0).astype(value.dtype)
    return lax.psum(kept, axis)


def shifted(block, axis, distance):
    devices = range(lax.axis_size(axis))
    route = [((i - distance) % len(devices), i) for i in devices]
    return lax.ppermute(block, axis, route)


def basis_pair(length, mode_count):
    position = jnp.arange(length, dtype=jnp.int32)
    wavenum = jnp.arange(mode_count, dtype=jnp.int32)
    angles = (position[:, None] * wavenum[None, :] % length).astype(jnp.float32) * (
        2.0 * math.pi / length
    )
    basis_cols = jnp.concatenate([jnp.cos(angles), jnp.sin(angles)], axis=1)
    weight = jnp.where(wavenum == 0, 1.0, 2.0).astype(jnp.float32) / length
    weight = jnp.concatenate([weight, weight])
    return (basis_cols * weight[None, :], basis_cols.T)


def mode_keep(levels_cut, mode_count):
    wavenum = jnp.tile(jnp.arange(mode_count, dtype=jnp.int32), 2)
    return (wavenum[None, :] <= levels_cut[:, None]).astype(jnp.float32)


def x_filter(columns, analysis_x, synthesis_x, keep_x):
    coeffs = (
        jnp.einsum("xk,czxj->czkj", analysis_x, columns, precision=highest)
        * keep_x[None, :, :, None]
    )
    return jnp.einsum("kx,czkj->czxj", synthesis_x, coeffs, precision=highest)


def on_device(velocity, cutoffs, plane_index, boundary_index):
    devices = lax.axis_size("slab")
    member_rows = velocity.shape[3]
    across = velocity.shape[4]
    along = member_rows * devices
    analysis_x, synthesis_x = basis_pair(along, KX)
    analysis_y, synthesis_y = basis_pair(across, KY)
    keep_x = mode_keep(cutoffs[0, 0], KX)
    keep_y = mode_keep(cutoffs[0, 1], KY)
    own_field = velocity[0]
    spectra = (
        jnp.einsum("czxy,yj->czxj", own_field, analysis_y, precision=highest)
        * keep_y[None, :, None, :]
    )
    columns = lax.all_to_all(spectra, "slab", split_axis=3, concat_axis=2, tiled=True)
    smooth = x_filter(columns, analysis_x, synthesis_x, keep_x)
    returned = lax.all_to_all(smooth, "slab", split_axis=2, concat_axis=3, tiled=True)
    result = jnp.einsum("czxj,jy->czxy", returned, synthesis_y, precision=highest)
    first_row = lax.axis_index("slab") * member_rows
    local_index = jnp.clip(plane_index[0] - first_row, 0, member_rows - 1)
    plane_part = lax.dynamic_index_in_dim(result, local_index, 2, keepdims=False)
    source_plane = spread(plane_part, "slab", plane_index[0] // member_rows)
    inflow = shifted(source_plane, "ens", 1)
    streamwise = first_row + jnp.arange(member_rows, dtype=jnp.int32)
    offset = jnp.abs(streamwise - boundary_index[0])
    distance = jnp.minimum(offset, along - offset)
    relax = jnp.exp(-distance.astype(jnp.float32) / (along / 4.0))
    weight = relax[None, None, :, None]
    blended = result + weight * (inflow[:, :, None, :] - result)
    return blended[None]


def solution(mesh):
    in_specs = (P("ens", None, None, "slab", None), P("ens", None, None), P("ens"), P("ens"))
    out_specs = P("ens", None, None, "slab", None)
    return jax.shard_map(
        on_device, mesh=mesh, in_specs=in_specs, out_specs=out_specs, check_vma=False
    )
```

profile of v0, /device:TPU:8, one launch (start us, length us, event | category | flops | bytes accessed | tf_op | source)
XLA Modules:
  0.0 1089.4 jit_solution(2496585179114449928)
XLA Ops:
  6.5 4.1 fusion.37
  10.7 0.8 slice_bitcast_fusion
  11.4 0.1 compare_convert_fusion.1
  11.5 84.5 %bitcast_multiply_fusion = f32[3,8,256,512]{2,3,1,0:T(8,128)} fusion(f32[8,512]{1,0:T(8,128)S(1)} %compare_convert_fusion.1, f32[1,3,8,256,1024]{4,3,2,1,0:T(8,128)} %param.4, f32[1024,256]{1,0:T(8,128)S(1)} %get-tuple-element.7, f32[1024,256]{1,0:T(8,128)S(1)} %get-tuple-element.8, f32[512]{0:T(512)S(1)} %pad_maximum_fusion.7), kind=kOutput, calls=%fused_computation.3 | convolution fusion | flops 38658899968 | bytes 39864320 | tf_op jit(solution)/shard_map/czxy,yj->czxj/dot_general | solution.py:59
  96.0 16.3 %copy.17 = f32[3,8,256,512]{2,1,0,3:T(8,128)} copy(f32[3,8,256,512]{2,3,1,0:T(8,128)} %bitcast_multiply_fusion) | data formatting | bytes 25165824 | tf_op jit(solution)/shard_map/mul | solution.py:59
  112.3 5.5 all-to-all-start
  117.9 0.1 compare_convert_fusion
  118.0 17.5 %fusion.27 = (f32[2048,512]{1,0:T(8,128)}, f32[2048,512]{1,0:T(8,128)}) fusion(), kind=kLoop, calls=%fused_computation.29 | loop fusion | flops 14680064 | bytes 8388608 | tf_op jit(solution)/shard_map/sin | solution.py:29
  135.6 252.6 %all-to-all-done = f32[3,8,256,512]{2,1,0,3:T(8,128)} async-done(((f32[3,8,256,512]{2,1,0,3:T(8,128)}), f32[3,8,256,512]{2,1,0,3:T(8,128)}, u32[]{:S(2)}, u32[]{:S(2)}) %all-to-all-start) | async-done | bytes 12582944 | tf_op jit(solution)/shard_map/all_to_all | solution.py:62
  388.1 16.6 %copy.36 = f32[3,8,256,8,64]{2,3,4,1,0:T(8,128)} copy(f32[3,8,256,8,64]{2,1,0,4,3:T(8,128)} %bitcast.4) | data formatting | bytes 25165824 | tf_op jit(solution)/shard_map/all_to_all | solution.py:62
  404.8 13.6 %all_to_all.29 = f32[3,8,2048,64]{2,3,1,0:T(8,128)} reshape(f32[3,8,8,256,64]{3,2,4,1,0:T(8,128)} %bitcast.77) | data formatting | bytes 25165824 | tf_op jit(solution)/shard_map/all_to_all | solution.py:62
  418.4 47.2 %fusion.4 = f32[3,8,64,1024]{3,2,1,0:T(8,128)} fusion(f32[3,8,2048,64]{2,3,1,0:T(8,128)} %all_to_all.29, f32[2048,512]{1,0:T(8,128)} %get-tuple-element.9, f32[2048,512]{1,0:T(8,128)} %get-tuple-element.10, f32[1024]{0:T(1024)S(1)} %pad_maximum_fusion.6), kind=kOutput, calls=%fused_computation.8 | convolution fusion | flops 38658899968 | bytes 27267072 | tf_op jit(solution)/shard_map/xk,czxj->czkj/dot_general | solution.py:42
  465.6 0.0 copy-done.2
  465.6 44.3 %fusion.9 = f32[3,8,2048,64]{2,3,1,0:T(8,128)} fusion(f32[2048,512]{1,0:T(8,128)S(1)} %copy-done.1, f32[2048,512]{1,0:T(8,128)S(1)} %copy-done.2, f32[3,8,64,1024]{3,2,1,0:T(8,128)} %fusion.4, f32[8,1024]{1,0:T(8,128)S(1)} %compare_convert_fusion), kind=kOutput, calls=%fused_computation.16 | convolution fusion | flops 38658375680 | bytes 27295744 | tf_op jit(solution)/shard_map/kx,czkj->czxj/dot_general | solution.py:45
  509.9 17.7 %copy.19 = f32[3,8,2048,64]{3,1,0,2:T(8,128)} copy(f32[3,8,2048,64]{2,3,1,0:T(8,128)} %fusion.9) | data formatting | bytes 25165824 | tf_op jit(solution)/shard_map/kx,czkj->czxj/transpose | solution.py:45
  527.6 20.5 %reshape.91 = f32[8,1,393216]{2,1,0:T(1,128)} reshape(f32[2048,3,8,64]{3,2,1,0:T(8,128)} %bitcast.74) | data formatting | bytes 25165824
  548.1 8.8 all-to-all-start.1
  557.6 269.6 %all-to-all-done.1 = f32[8,1,393216]{2,1,0:T(1,128)} async-done(((f32[8,1,393216]{2,1,0:T(1,128)}), f32[8,1,393216]{2,1,0:T(1,128)}, u32[]{:S(2)}, u32[]{:S(2)}) %all-to-all-start.1) | async-done | bytes 12582944 | tf_op jit(solution)/shard_map/all_to_all | solution.py:64
  827.2 0.5 broadcast.88
  827.7 36.8 %reduce = f32[8,393216]{1,0:T(8,128)} reduce(f32[8,1,393216]{2,1,0:T(1,128)} %all-to-all-done.1, f32[]{:T(128)} %broadcast.88), dimensions={1}, to_apply=%all_to_all.30.reduce_sub_computation | reduce | bytes 25165828 | tf_op jit(solution)/shard_map/all_to_all | solution.py:64
  864.5 23.2 %reshape.92 = f32[2048,3,8,64]{3,2,1,0:T(8,128)} reshape(f32[8,393216]{1,0:T(8,128)} %reduce) | data formatting | bytes 25165824
  887.7 18.7 %copy.21 = f32[3,8,256,8,64]{2,4,3,1,0:T(8,128)} copy(f32[3,8,256,8,64]{4,1,0,2,3:T(8,128)} %bitcast.75) | data formatting | bytes 25165824 | tf_op jit(solution)/shard_map/all_to_all | solution.py:64
  906.4 85.2 %fusion.24 = f32[3,8,256,1024]{3,2,1,0:T(8,128)S(1)} fusion(f32[3,8,256,512]{2,3,1,0:T(8,128)} %bitcast.76, f32[1024,256]{1,0:T(8,128)S(1)} %get-tuple-element.7, f32[1024,256]{1,0:T(8,128)S(1)} %get-tuple-element.8), kind=kOutput, calls=%fused_computation.26 | convolution fusion | flops 38655229952 | bytes 39845888 | tf_op jit(solution)/shard_map/czxj,jy->czxy/dot_general | solution.py:65
  991.5 0.0 copy-start
  991.6 8.9 copy-done
  1000.5 0.1 broadcast_select_fusion
  1000.6 0.7 copy.37
  1001.2 0.0 all-reduce.2.cloned.1.call-update
  1001.9 55.8 %all-reduce.2.cloned.1.call-done = f32[3,8,1024]{2,1,0:T(8,128)} async-done(((f32[3,8,1024]{2,1,0:T(8,128)}), f32[3,8,1024]{2,1,0:T(8,128)}) %all-reduce.2.cloned.1.call-update) | async-done | bytes 98320 | tf_op jit(solution)/shard_map/psum | solution.py:14
  1057.7 1.5 collective-permute-start
  1059.2 4.2 collective-permute-done
  1063.4 18.8 %add_bitcast_fusion = f32[1,3,8,256,1024]{4,3,2,1,0:T(8,128)} fusion(f32[3,8,256,1024]{3,2,1,0:T(8,128)} %copy-done, f32[3,8,1024]{2,1,0:T(8,128)S(1)} %collective-permute-done, f32[256]{0:T(256)S(1)} %fusion.42), kind=kLoop, calls=%fused_computation.2 | loop fusion | flops 18874368 | bytes 50430976 | tf_op jit(solution)/shard_map/broadcast_in_dim | solution.py:77
  (13 shorter events, 0.1 us)
Async XLA Ops:
  112.3 275.8 %all-to-all-start = ((f32[3,8,256,512]{2,1,0,3:T(8,128)}), f32[3,8,256,512]{2,1,0,3:T(8,128)}, u32[]{:S(2)}, u32[]{:S(2)}) async-start(f32[3,8,256,512]{2,1,0,3:T(8,128)} %copy.17), calls=%async_computation | async-start | bytes 25165824 | tf_op jit(solution)/shard_map/all_to_all | solution.py:62
  418.4 47.2 %copy-start.1 = (f32[2048,512]{1,0:T(8,128)S(1)}, f32[2048,512]{1,0:T(8,128)}, u32[]{:S(2)}) copy-start(f32[2048,512]{1,0:T(8,128)} %get-tuple-element.9) | copy-start | bytes 12582916
  418.4 47.2 %copy-start.2 = (f32[2048,512]{1,0:T(8,128)S(1)}, f32[2048,512]{1,0:T(8,128)}, u32[]{:S(2)}) copy-start(f32[2048,512]{1,0:T(8,128)} %get-tuple-element.10) | copy-start | bytes 12582916
  548.1 279.1 %all-to-all-start.1 = ((f32[8,1,393216]{2,1,0:T(1,128)}), f32[8,1,393216]{2,1,0:T(1,128)}, u32[]{:S(2)}, u32[]{:S(2)}) async-start(f32[8,1,393216]{2,1,0:T(1,128)} %reshape.91), calls=%async_computation.1 | async-start | bytes 25165824 | tf_op jit(solution)/shard_map/all_to_all | solution.py:64
  556.9 500.8 %all-reduce.2.cloned.1.call-start = ((), (), s32[]{:S(2)}) async-start(), calls=%async_computation.2 | async-start | bytes 196608 | tf_op jit(solution)/shard_map/psum | solution.py:14
  991.5 8.9 copy-start
  1057.7 5.7 collective-permute-start
Sparse Core Ops, SparseCore 0:
  1001.4 56.2 all-reduce.1
where the time goes:
time: 1090 us
  waiting for transfers between devices  582 us (53%)
  matrix products  261 us (24%)
  local copies, waits for them, and re-layouts  138 us (13%)
  other arithmetic  77.5 us (7%)
  starting transfers between devices  15.8 us (1%)
  between operations  15.2 us (1%)
    all_to_all x1, waiting for transfers between devices, on_device(): lax.all_to_all(smooth, 'slab', split_axis=2, concat_axis=3, tiled=True)  270 us
    all_to_all x1, waiting for transfers between devices, on_device(): lax.all_to_all(spectra, 'slab', split_axis=3, concat_axis=2, tiled=True)  253 us
    dot_general x1, matrix products, on_device(): jnp.einsum('czxj,jy->czxy', returned, synthesis_y, precision=highest)  85.2 us
    dot_general x1, matrix products, on_device(): jnp.einsum('czxy,yj->czxj', own_field, analysis_y, precision=highest)  84.5 us
    psum x1, waiting for transfers between devices, spread(): return lax.psum(kept, axis)  55.8 us
    unnamed x13, local copies, waits for them, and re-layouts  53.3 us
    dot_general x1, matrix products, x_filter(): jnp.einsum('xk,czxj->czkj', analysis_x, columns, precision=highest)  47.2 us
    dot_general x1, matrix products, x_filter(): return jnp.einsum('kx,czkj->czxj', synthesis_x, coeffs, precision=highest)  44.3 us
  transfers between devices with their start and end apart: 4, of which 4 were waited for; matrix products, arithmetic and copies ran while one was open for 2% of the time, Pallas kernels for 0%

commit v1 on v0

--- a/solution.py
+++ b/solution.py
@@ -1,3 +1,4 @@
+import functools
 import math
 import jax
 import jax.numpy as jnp
@@ -7,6 +8,21 @@
 KX = 512
 KY = 256
 highest = lax.Precision.HIGHEST
+
+
+def view_the_islands(slab_in, k_dim, dimension_no):
+    return jnp.concatenate(
+        lax.all_to_all(
+            jnp.stack(jnp.split(slab_in, lax.axis_size("slab"), axis=k_dim)),
+            axis_name="slab",
+            split_axis=0,
+            concat_axis=0,
+        ),
+        axis=dimension_no,
+    )
+
+
+pass_column_up = functools.partial(view_the_islands, k_dim=2, dimension_no=3)
 
 
 def spread(value, axis, source):
@@ -61,7 +77,7 @@
     )
     columns = lax.all_to_all(spectra, "slab", split_axis=3, concat_axis=2, tiled=True)
     smooth = x_filter(columns, analysis_x, synthesis_x, keep_x)
-    returned = lax.all_to_all(smooth, "slab", split_axis=2, concat_axis=3, tiled=True)
+    returned = pass_column_up(smooth)
     result = jnp.einsum("czxj,jy->czxy", returned, synthesis_y, precision=highest)
     first_row = lax.axis_index("slab") * member_rows
     local_index = jnp.clip(plane_index[0] - first_row, 0, member_rows - 1)

time: 1090 us -> 999 us (0.917)
  local copies, waits for them, and re-layouts: 138 us -> 79.1 us
  other arithmetic: 77.5 us -> 40.7 us
    all_to_all x1 -> x0, other arithmetic: 36.8 us -> none  [on_device(): lax.all_to_all(smooth, 'slab', split_axis=2, concat_axis=3, tiled=True)]
    unnamed x13 -> x18, local copies, waits for them, and re-layouts: 53.3 us -> 18.8 us
    all_to_all x2 -> x0, local copies, waits for them, and re-layouts: 19.2 us -> none  [on_device(): lax.all_to_all(smooth, 'slab', split_axis=2, concat_axis=3, tiled=True)]
    transpose x1 -> x0, local copies, waits for them, and re-layouts: 17.7 us -> none  [x_filter(): return jnp.einsum('kx,czkj->czxj', synthesis_x, coeffs, precision=highest)]
    reshape x0 -> x1, local copies, waits for them, and re-layouts: none -> 11.5 us  [view_the_islands(): jnp.concatenate(lax.all_to_all(jnp.stack(jnp.split(slab_in, lax.axis_size...]
where the time goes in v1:
time: 999 us; the launch traced here: 994 us
  waiting for transfers between devices  582 us (58%)
  matrix products  261 us (26%)
  local copies, waits for them, and re-layouts  79.1 us (8%)
  other arithmetic  40.7 us (4%)
  starting transfers between devices  15.8 us (2%)
  between operations  15 us (2%)
    all_to_all x1, waiting for transfers between devices, view_the_islands(): lax.all_to_all(jnp.stack(jnp.split(slab_in, lax.axis_size('slab'), axis=k...  270 us
    all_to_all x1, waiting for transfers between devices, on_device(): lax.all_to_all(spectra, 'slab', split_axis=3, concat_axis=2, tiled=True)  253 us
    dot_general x1, matrix products, on_device(): jnp.einsum('czxj,jy->czxy', returned, synthesis_y, precision=highest)  85.1 us
    dot_general x1, matrix products, on_device(): jnp.einsum('czxy,yj->czxj', own_field, analysis_y, precision=highest)  84.4 us
    psum x1, waiting for transfers between devices, spread(): return lax.psum(kept, axis)  55.8 us
    dot_general x1, matrix products, x_filter(): jnp.einsum('xk,czxj->czkj', analysis_x, columns, precision=highest)  47.4 us
    dot_general x1, matrix products, x_filter(): return jnp.einsum('kx,czkj->czxj', synthesis_x, coeffs, precision=highest)  44.3 us
    all_to_all x2, local copies, waits for them, and re-layouts, on_device(): lax.all_to_all(spectra, 'slab', split_axis=3, concat_axis=2, tiled=True)  30.3 us
  transfers between devices with their start and end apart: 4, of which 4 were waited for; matrix products, arithmetic and copies ran while one was open for 2% of the time, Pallas kernels for 0%

profile of v1, /device:TPU:8, one launch (start us, length us, event | category | flops | bytes accessed | tf_op | source)
XLA Modules:
  0.0 994.1 jit_solution(18424202729167941049)
XLA Ops:
  6.5 4.1 fusion.45
  10.7 0.8 slice_bitcast_fusion.8
  11.4 0.1 compare_convert_fusion.1
  11.5 84.4 %bitcast_multiply_fusion = f32[3,8,256,512]{2,3,1,0:T(8,128)} fusion(f32[8,512]{1,0:T(8,128)S(1)} %compare_convert_fusion.1, f32[1,3,8,256,1024]{4,3,2,1,0:T(8,128)} %param.4, f32[1024,256]{1,0:T(8,128)S(1)} %get-tuple-element.7, f32[1024,256]{1,0:T(8,128)S(1)} %get-tuple-element.8, f32[512]{0:T(512)S(1)} %pad_maximum_fusion.7), kind=kOutput, calls=%fused_computation.3 | convolution fusion | flops 38658899968 | bytes 39864320 | tf_op jit(solution)/shard_map/czxy,yj->czxj/dot_general | solution.py:75
  95.9 16.3 %copy.11 = f32[3,8,256,512]{2,1,0,3:T(8,128)} copy(f32[3,8,256,512]{2,3,1,0:T(8,128)} %bitcast_multiply_fusion) | data formatting | bytes 25165824 | tf_op jit(solution)/shard_map/mul | solution.py:75
  112.2 5.6 all-to-all-start
  117.8 0.1 compare_convert_fusion
  117.9 17.5 %fusion.27 = (f32[2048,512]{1,0:T(8,128)}, f32[2048,512]{1,0:T(8,128)}) fusion(), kind=kLoop, calls=%fused_computation.29 | loop fusion | flops 14680064 | bytes 8388608 | tf_op jit(solution)/shard_map/sin | solution.py:45
  135.4 252.6 %all-to-all-done = f32[3,8,256,512]{2,1,0,3:T(8,128)} async-done(((f32[3,8,256,512]{2,1,0,3:T(8,128)}), f32[3,8,256,512]{2,1,0,3:T(8,128)}, u32[]{:S(2)}, u32[]{:S(2)}) %all-to-all-start) | async-done | bytes 12582944 | tf_op jit(solution)/shard_map/all_to_all | solution.py:78
  388.0 16.6 %copy.26 = f32[3,8,256,8,64]{2,3,4,1,0:T(8,128)} copy(f32[3,8,256,8,64]{2,1,0,4,3:T(8,128)} %bitcast.4) | data formatting | bytes 25165824 | tf_op jit(solution)/shard_map/all_to_all | solution.py:78
  404.7 13.6 %all_to_all.19 = f32[3,8,2048,64]{2,3,1,0:T(8,128)} reshape(f32[3,8,8,256,64]{3,2,4,1,0:T(8,128)} %bitcast.102) | data formatting | bytes 25165824 | tf_op jit(solution)/shard_map/all_to_all | solution.py:78
  418.3 47.4 %fusion.4 = f32[3,8,64,1024]{3,2,1,0:T(8,128)} fusion(f32[3,8,2048,64]{2,3,1,0:T(8,128)} %all_to_all.19, f32[2048,512]{1,0:T(8,128)} %get-tuple-element.9, f32[2048,512]{1,0:T(8,128)} %get-tuple-element.10, f32[1024]{0:T(1024)S(1)} %pad_maximum_fusion.6), kind=kOutput, calls=%fused_computation.8 | convolution fusion | flops 38658899968 | bytes 27267072 | tf_op jit(solution)/shard_map/xk,czxj->czkj/dot_general | solution.py:58
  465.7 44.3 %fusion.9 = f32[3,8,2048,64]{2,3,1,0:T(8,128)S(1)} fusion(f32[2048,512]{1,0:T(8,128)S(1)} %copy-done.1, f32[2048,512]{1,0:T(8,128)S(1)} %copy-done.2, f32[3,8,64,1024]{3,2,1,0:T(8,128)} %fusion.4, f32[8,1024]{1,0:T(8,128)S(1)} %compare_convert_fusion), kind=kOutput, calls=%fused_computation.16 | convolution fusion | flops 38658375680 | bytes 27295744 | tf_op jit(solution)/shard_map/kx,czkj->czxj/dot_general | solution.py:61
  510.1 1.3 fusion.37
  511.4 1.3 fusion.36
  512.7 1.3 fusion.35
  514.0 1.3 fusion.34
  515.4 1.3 fusion.33
  516.7 1.3 fusion.32
  518.0 1.3 fusion.31
  519.3 1.3 fusion.30
  520.6 8.8 all-to-all-start.1
  530.1 269.6 %all-to-all-done.1 = f32[8,3,8,256,64]{3,4,2,1,0:T(8,128)} async-done(((f32[8,3,8,256,64]{3,4,2,1,0:T(8,128)}), f32[8,3,8,256,64]{3,4,2,1,0:T(8,128)}, u32[]{:S(2)}, u32[]{:S(2)}) %all-to-all-start.1) | async-done | bytes 12582944 | tf_op jit(solution)/shard_map/all_to_all | solution.py:15
  799.7 11.5 %copy.13 = f32[3,8,256,8,64]{2,4,3,1,0:T(8,128)} copy(f32[3,8,256,8,64]{2,4,1,0,3:T(8,128)} %bitcast.21) | data formatting | bytes 25165824 | tf_op jit(solution)/shard_map/reshape | solution.py:14
  811.2 85.1 %fusion.24 = f32[3,8,256,1024]{3,2,1,0:T(8,128)S(1)} fusion(f32[3,8,256,512]{2,3,1,0:T(8,128)} %bitcast.101, f32[1024,256]{1,0:T(8,128)S(1)} %get-tuple-element.7, f32[1024,256]{1,0:T(8,128)S(1)} %get-tuple-element.8), kind=kOutput, calls=%fused_computation.26 | convolution fusion | flops 38655229952 | bytes 39845888 | tf_op jit(solution)/shard_map/czxj,jy->czxy/dot_general | solution.py:81
  896.4 8.9 copy-done
  905.3 0.1 broadcast_select_fusion
  905.4 0.7 copy.27
  906.7 55.8 %all-reduce.2.cloned.1.call-done = f32[3,8,1024]{2,1,0:T(8,128)} async-done(((f32[3,8,1024]{2,1,0:T(8,128)}), f32[3,8,1024]{2,1,0:T(8,128)}) %all-reduce.2.cloned.1.call-update) | async-done | bytes 98320 | tf_op jit(solution)/shard_map/psum | solution.py:30
  962.6 1.5 collective-permute-start
  964.0 4.2 collective-permute-done
  968.3 18.8 %add_bitcast_fusion = f32[1,3,8,256,1024]{4,3,2,1,0:T(8,128)} fusion(f32[3,8,256,1024]{3,2,1,0:T(8,128)} %copy-done, f32[3,8,1024]{2,1,0:T(8,128)S(1)} %collective-permute-done, f32[256]{0:T(256)S(1)} %fusion.50), kind=kLoop, calls=%fused_computation.2 | loop fusion | flops 18874368 | bytes 50430976 | tf_op jit(solution)/shard_map/broadcast_in_dim | solution.py:93
  (16 shorter events, 0.1 us)
Async XLA Ops:
  112.2 275.8 %all-to-all-start = ((f32[3,8,256,512]{2,1,0,3:T(8,128)}), f32[3,8,256,512]{2,1,0,3:T(8,128)}, u32[]{:S(2)}, u32[]{:S(2)}) async-start(f32[3,8,256,512]{2,1,0,3:T(8,128)} %copy.11), calls=%async_computation | async-start | bytes 25165824 | tf_op jit(solution)/shard_map/all_to_all | solution.py:78
  418.3 47.4 %copy-start.1 = (f32[2048,512]{1,0:T(8,128)S(1)}, f32[2048,512]{1,0:T(8,128)}, u32[]{:S(2)}) copy-start(f32[2048,512]{1,0:T(8,128)} %get-tuple-element.9) | copy-start | bytes 12582916
  418.3 47.4 %copy-start.2 = (f32[2048,512]{1,0:T(8,128)S(1)}, f32[2048,512]{1,0:T(8,128)}, u32[]{:S(2)}) copy-start(f32[2048,512]{1,0:T(8,128)} %get-tuple-element.10) | copy-start | bytes 12582916
  520.6 279.1 %all-to-all-start.1 = ((f32[8,3,8,256,64]{3,4,2,1,0:T(8,128)}), f32[8,3,8,256,64]{3,4,2,1,0:T(8,128)}, u32[]{:S(2)}, u32[]{:S(2)}) async-start(f32[8,3,8,256,64]{3,4,2,1,0:T(8,128)} %fusion.30), calls=%async_computation.1 | async-start | bytes 25165824 | tf_op jit(solution)/shard_map/all_to_all | solution.py:15
  529.4 433.1 %all-reduce.2.cloned.1.call-start = ((), (), s32[]{:S(2)}) async-start(), calls=%async_computation.2 | async-start | bytes 196608 | tf_op jit(solution)/shard_map/psum | solution.py:30
  896.4 8.9 copy-start
  962.6 5.7 collective-permute-start
Sparse Core Ops, SparseCore 0:
  906.2 56.2 all-reduce.1
